TPU v7x, 128 devices: a whole 4x4x4 slice. The times are simulated.
128 devices in a mesh: gx: 8 (over y, z_lo), gy: 4 (over x), gz: 4 (over z_hi, core).
Axes of the slice: x: 4, y: 4, z: 4 (z_hi: 2, z_lo: 2; z = z_hi * 2 + z_lo), core: 2. Of those that a mesh axis runs over, the one named last changes fastest.
Arguments:
- targets: float32 [512, 512, 512], P('gx', 'gy', 'gz'), may hold values from -6 to 6
- basis_first: float32 [512, 512], replicated, may hold values from -0.25 to 0.25
- basis_second: float32 [512, 512], replicated, may hold values from -0.25 to 0.25
- basis_third: float32 [512, 512], replicated, may hold values from -0.25 to 0.25
- eigen_first: float32 [512], replicated, may hold values from 0.1 to 1
- eigen_second: float32 [512], replicated, may hold values from 0.1 to 1
- eigen_third: float32 [512], replicated, may hold values from 0.1 to 1
- noise: float32 [1], replicated, may hold values from 0.5 to 1
Outputs:
- weights: float32 [512, 512, 512], P('gx', 'gy', 'gz')
All inputs are finite; a program needn't handle non-finite values.
Results may differ from a plain program's by a relative error of at most 0.000071.
Values sent between devices are 32-bit elements; how exact they have to be, the bound alone decides.
A program may use at most 64 MiB of HBM per device.

v0:
```python
import jax
import jax.numpy as jnp
from jax import lax
from jax.sharding import Mesh
from jax.sharding import PartitionSpec as P

GZ = ("gz_0", "gz_1")
GX_GZ = ("gx", "gz_0", "gz_1")


def split_up(shard, dim, count):
    lengths = shard.shape
    pieces = shard.reshape(*lengths[:dim], count, lengths[dim] // count, *lengths[dim + 1 :])
    return jnp.moveaxis(pieces, dim, 0)


def in_order(pieces, dim):
    pieces = jnp.moveaxis(pieces, 0, dim)
    lengths = pieces.shape
    return pieces.reshape(*lengths[:dim], lengths[dim] * lengths[dim + 1], *lengths[dim + 2 :])


def turned_blocks(pieces, axes, turns):
    inside = pieces.shape[1:]
    result = pieces.reshape(*(lax.axis_size(a) for a in axes), *inside)
    for k in turns:
        result = lax.all_to_all(result, axes[k], k, k, tiled=True)
    return result.reshape(-1, *inside)


def exchange_by_chip(shard, groups, turns, split_dim, concat_dim):
    count = lax.axis_size(groups[0]) * lax.axis_size(groups[1])
    pieces = split_up(shard, split_dim, count)
    return in_order(turned_blocks(pieces, groups, turns), concat_dim)


def per_device(
    targets, basis_first, basis_second, basis_third, eigen_first, eigen_second, eigen_third, noise
):
    high = lax.Precision.HIGHEST
    count_z = lax.axis_size(GZ)
    full_one = basis_first.shape[0]
    full_three = basis_third.shape[0]
    block = lax.all_to_all(targets, GZ, split_axis=0, concat_axis=2, tiled=True)
    lead, middle = (block.shape[0], block.shape[1])
    block = jnp.dot(block.reshape(-1, full_three), basis_third, precision=high).reshape(
        lead, middle, full_three
    )
    block = lax.all_to_all(block, "gy", split_axis=2, concat_axis=1, tiled=True)
    block = jnp.einsum("ajc,jb->abc", block, basis_second, precision=high)
    block = lax.all_to_all(block, GX_GZ, split_axis=1, concat_axis=0, tiled=True)
    width_two, width_three = (block.shape[1], block.shape[2])
    flat = block.reshape(full_one, -1)
    rotated = jnp.dot(basis_first.T, flat, precision=high).reshape(full_one, width_two, width_three)
    start_two = (lax.axis_index("gx") * count_z + lax.axis_index(GZ)) * width_two
    start_three = lax.axis_index("gy") * width_three
    local_two = lax.dynamic_slice_in_dim(eigen_second, start_two, width_two, 0)
    local_three = lax.dynamic_slice_in_dim(eigen_third, start_three, width_three, 0)
    spectrum = (
        eigen_first[:, None, None] * local_two[None, :, None] * local_three[None, None, :]
        + noise[0]
    )
    scaled = rotated / spectrum
    result = jnp.dot(basis_first, scaled.reshape(full_one, -1), precision=high).reshape(
        full_one, width_two, width_three
    )
    result = lax.all_to_all(result, GX_GZ, split_axis=0, concat_axis=1, tiled=True)
    result = jnp.einsum("abc,jb->ajc", result, basis_second, precision=high)
    result = lax.all_to_all(result, "gy", split_axis=1, concat_axis=2, tiled=True)
    lead, middle = (result.shape[0], result.shape[1])
    result = jnp.dot(result.reshape(-1, full_three), basis_third.T, precision=high).reshape(
        lead, middle, full_three
    )
    return exchange_by_chip(result, ("gz_0", "gz_1"), (1, 0), 2, 0)


def solution(mesh):
    finer = Mesh(
        mesh.devices.reshape(mesh.shape["gx"], mesh.shape["gy"], 2, 2), ("gx", "gy", "gz_0", "gz_1")
    )
    in_specs = (P("gx", "gy", GZ), P(), P(), P(), P(), P(), P(), P())
    out_specs = P("gx", "gy", GZ)
    return jax.shard_map(
        per_device, mesh=finer, in_specs=in_specs, out_specs=out_specs, check_vma=False
    )
```

profile of v0, /device:TPU:33, one launch (start us, length us, event | category | flops | bytes accessed | tf_op | source)
XLA Modules:
  0.0 456.0 jit_solution(10488020226703077780)
XLA Ops:
  0.0 53.7 %all_to_all.91 = f32[64,128,128]{2,1,0:T(8,128)S(1)} all-to-all(f32[64,128,128]{2,1,0:T(8,128)} %param.8), channel_id=1, replica_groups=mesh['gx'=8,'gy'=4,'gz_0'=2,'gz_1'=2] {'gz_0','gz_1'}, dimensions={0} | all-to-all | bytes 8388608 | tf_op jit(solution)/shard_map/all_to_all | solution.py:44
  53.7 4.8 %copy.65 = f32[4,16,128,128]{3,0,2,1:T(4,128)} copy(f32[4,16,128,128]{3,2,1,0:T(8,128)S(1)} %bitcast.83) | data formatting | bytes 8388608 | tf_op jit(solution)/shard_map/all_to_all | solution.py:44
  58.5 5.5 %dot_general.28 = f32[16,128,512]{2,1,0:T(8,128)} reshape(f32[16,128,4,128]{3,2,1,0:T(4,128)} %bitcast.75) | data formatting | bytes 8388608 | tf_op jit(solution)/shard_map/dot_general | solution.py:46
  63.9 9.8 %fusion.11 = f32[16,128,512]{2,1,0:T(8,128)} fusion(f32[16,128,512]{2,1,0:T(8,128)} %dot_general.28, f32[512,512]{1,0:T(8,128)S(1)} %copy-done), kind=kOutput, calls=%fused_computation.15 | convolution fusion | flops 6442450944 | bytes 9437184 | tf_op jit(solution)/shard_map/dot_general | solution.py:46
  73.8 5.4 %copy.37 = f32[16,128,512]{1,0,2:T(8,128)} copy(f32[16,128,512]{2,1,0:T(8,128)} %fusion.11) | data formatting | bytes 8388608 | tf_op jit(solution)/shard_map/dot_general | solution.py:46
  79.2 51.5 %all_to_all.92 = f32[16,128,512]{1,0,2:T(8,128)S(1)} all-to-all(f32[16,128,512]{1,0,2:T(8,128)} %copy.37), channel_id=1, replica_groups=mesh['gx'=8,'gy'=4,'gz_0'=2,'gz_1'=2] {'gy'}, dimensions={2} | all-to-all | bytes 8388608 | tf_op jit(solution)/shard_map/all_to_all | solution.py:49
  130.7 4.7 %copy.64 = f32[16,128,4,128]{1,2,3,0:T(4,128)} copy(f32[16,128,4,128]{1,0,3,2:T(8,128)S(1)} %bitcast.76) | data formatting | bytes 8388608 | tf_op jit(solution)/shard_map/all_to_all | solution.py:49
  135.4 5.5 %all_to_all.71 = f32[16,512,128]{1,2,0:T(8,128)} reshape(f32[16,4,128,128]{2,1,3,0:T(4,128)} %bitcast.77) | data formatting | bytes 8388608 | tf_op jit(solution)/shard_map/all_to_all | solution.py:49
  140.9 9.8 %convolution_bitcast_fusion.1 = f32[16,512,128]{1,2,0:T(8,128)} fusion(f32[16,512,128]{1,2,0:T(8,128)} %all_to_all.71, f32[512,512]{1,0:T(8,128)S(1)} %copy-done.1), kind=kOutput, calls=%fused_computation.12 | convolution fusion | flops 6442450944 | bytes 9437184 | tf_op jit(solution)/shard_map/ajc,jb->abc/dot_general | solution.py:50
  150.7 5.5 %copy.39 = f32[16,512,128]{2,0,1:T(8,128)} copy(f32[16,512,128]{1,2,0:T(8,128)} %convolution_bitcast_fusion.1) | data formatting | bytes 8388608 | tf_op jit(solution)/shard_map/ajc,jb->abc/transpose | solution.py:50
  156.2 9.0 %all-to-all-start.2 = ((f32[16,512,128]{2,0,1:T(8,128)}), f32[16,512,128]{2,0,1:T(8,128)}, u32[]{:S(2)}, u32[]{:S(2)}) async-start(f32[16,512,128]{2,0,1:T(8,128)} %copy.39), calls=%async_computation.2 | async-start | bytes 8388608 | tf_op jit(solution)/shard_map/all_to_all | solution.py:51
  167.4 46.8 %all-to-all-done.2 = f32[16,512,128]{2,0,1:T(8,128)} async-done(((f32[16,512,128]{2,0,1:T(8,128)}), f32[16,512,128]{2,0,1:T(8,128)}, u32[]{:S(2)}, u32[]{:S(2)}) %all-to-all-start.2) | async-done | bytes 4194336 | tf_op jit(solution)/shard_map/all_to_all | solution.py:51
  218.2 8.2 %fusion.6 = f32[512,2048]{0,1:T(8,128)S(1)} fusion(f32[512,512]{1,0:T(8,128)S(1)} %copy-done.2, f32[64,8,16,128]{3,2,1,0:T(8,128)S(1)} %bitcast.74, f32[]{:T(128)} %bitcast.71, f32[2048]{0:T(1024)S(1)} %broadcast_bitcast_fusion, f32[512,16]{0,1:T(8,128)S(1)} %broadcast_multiply_fusion), kind=kOutput, calls=%fused_computation.7 | convolution fusion | flops 6445596672 | bytes 9478148 | tf_op jit(solution)/shard_map/dot_general | solution.py:54
  226.4 8.4 %fusion.13 = f32[2048,512]{1,0:T(8,128)} fusion(f32[512,2048]{0,1:T(8,128)S(1)} %fusion.6, f32[512,512]{1,0:T(8,128)S(1)} %copy-done.2), kind=kOutput, calls=%fused_computation.19 | convolution fusion | flops 6442450944 | bytes 9437184 | tf_op jit(solution)/shard_map/dot_general | solution.py:64
  234.9 5.4 %copy.42 = f32[512,16,128]{2,1,0:T(8,128)} copy(f32[512,16,128]{0,2,1:T(8,128)} %bitcast.73) | data formatting | bytes 8388608 | tf_op jit(solution)/shard_map/reshape | solution.py:64
  240.3 61.1 %all_to_all.93 = f32[512,16,128]{2,1,0:T(8,128)S(1)} all-to-all(f32[512,16,128]{2,1,0:T(8,128)} %copy.42), channel_id=1, replica_groups=mesh['gx'=8,'gy'=4,'gz_0'=2,'gz_1'=2] {'gx','gz_0','gz_1'}, dimensions={0} | all-to-all | bytes 8388608 | tf_op jit(solution)/shard_map/all_to_all | solution.py:67
  301.9 14.7 %convolution_bitcast_fusion = f32[16,512,128]{1,2,0:T(8,128)} fusion(f32[16,512,128]{2,1,0:T(8,128)S(1)} %bitcast.79, f32[512,512]{1,0:T(8,128)S(1)} %copy-done.1), kind=kOutput, calls=%fused_computation.11 | convolution fusion | flops 6442450944 | bytes 9437184 | tf_op jit(solution)/shard_map/abc,jb->ajc/dot_general | solution.py:68
  316.6 5.4 %copy.45 = f32[16,512,128]{2,0,1:T(8,128)} copy(f32[16,512,128]{1,2,0:T(8,128)} %convolution_bitcast_fusion) | data formatting | bytes 8388608 | tf_op jit(solution)/shard_map/abc,jb->ajc/transpose | solution.py:68
  322.0 52.5 %all_to_all.94 = f32[16,512,128]{2,0,1:T(8,128)S(1)} all-to-all(f32[16,512,128]{2,0,1:T(8,128)} %copy.45), channel_id=1, replica_groups=mesh['gx'=8,'gy'=4,'gz_0'=2,'gz_1'=2] {'gy'}, dimensions={1} | all-to-all | bytes 8388608 | tf_op jit(solution)/shard_map/all_to_all | solution.py:69
  374.5 4.7 %copy.63 = f32[16,4,128,128]{3,1,2,0:T(4,128)} copy(f32[16,4,128,128]{3,0,2,1:T(8,128)S(1)} %bitcast.80) | data formatting | bytes 8388608 | tf_op jit(solution)/shard_map/all_to_all | solution.py:69
  379.2 5.5 %reshape.62 = f32[16,128,512,1]{2,1,0,3:T(8,128)} reshape(f32[16,128,4,128]{3,2,1,0:T(4,128)} %bitcast.81) | data formatting | bytes 8388608 | tf_op jit(solution)/shard_map/dot_general | solution.py:71
  384.7 8.6 %fusion.3 = f32[16,128,4,128]{3,1,2,0:T(8,128)S(1)} fusion(f32[4,128,512,1]{2,1,0,3:T(8,128)S(1)} %bitcast.72, f32[16,128,512,1]{2,1,0,3:T(8,128)} %reshape.62), kind=kOutput, calls=%fused_computation.3 | convolution fusion | flops 6442450944 | bytes 9437184 | tf_op jit(solution)/shard_map/dot_general | solution.py:71
  393.7 8.0 %all_to_all.95 = f32[2,2,16,128,128]{4,3,0,2,1:T(8,128)S(1)} all-to-all(f32[2,2,16,128,128]{4,3,0,2,1:T(8,128)S(1)} %copy.47), channel_id=1, replica_groups=mesh['gx'=8,'gy'=4,'gz_0'=2,'gz_1'=2] {'gz_1'}, dimensions={1} | all-to-all | bytes 8388608 | tf_op jit(solution)/shard_map/all_to_all | solution.py:27
  402.2 51.3 %all_to_all.96 = f32[2,2,16,128,128]{4,3,1,2,0:T(8,128)S(1)} all-to-all(f32[2,2,16,128,128]{4,3,1,2,0:T(8,128)S(1)} %copy.48), channel_id=1, replica_groups=mesh['gx'=8,'gy'=4,'gz_0'=2,'gz_1'=2] {'gz_0'}, dimensions={0} | all-to-all | bytes 8388608 | tf_op jit(solution)/shard_map/all_to_all | solution.py:27
  (17 shorter events, 9.3 us)
Async XLA Ops:
  0.0 63.9 %copy-start = (f32[512,512]{1,0:T(8,128)S(1)}, f32[512,512]{1,0:T(8,128)}, u32[]{:S(2)}) copy-start(f32[512,512]{1,0:T(8,128)} %param.11) | copy-start | bytes 3145732
  135.4 5.6 %copy-start.1 = (f32[512,512]{1,0:T(8,128)S(1)}, f32[512,512]{1,0:T(8,128)}, u32[]{:S(2)}) copy-start(f32[512,512]{1,0:T(8,128)} %param.10) | copy-start | bytes 3145732
  156.2 11.1 %copy-start.3 = (f32[512]{0:T(512)S(1)}, f32[512]{0:T(512)}, u32[]{:S(2)}) copy-start(f32[512]{0:T(512)} %param.12) | copy-start | bytes 6148
  156.2 58.0 %all-to-all-start.2 = ((f32[16,512,128]{2,0,1:T(8,128)}), f32[16,512,128]{2,0,1:T(8,128)}, u32[]{:S(2)}, u32[]{:S(2)}) async-start(f32[16,512,128]{2,0,1:T(8,128)} %copy.39), calls=%async_computation.2 | async-start | bytes 8388608 | tf_op jit(solution)/shard_map/all_to_all | solution.py:51
  214.2 4.0 copy-start.2
where the time goes:
time: 465 us; the launch traced here: 456 us
  blocking collectives  278 us (60%)
  local copies, waits for them, and re-layouts  61.7 us (13%)
  matrix products  59.5 us (13%)
  waiting for transfers between devices  46.8 us (10%)
  starting transfers between devices  8.96 us (2%)
    all_to_all x1, blocking collectives, per_device(): lax.all_to_all(result, GX_GZ, split_axis=0, concat_axis=1, tiled=True)  61.1 us
    all_to_all x2, blocking collectives, turned_blocks(): result = lax.all_to_all(result, axes[k], k, k, tiled=True)  59.2 us
    all_to_all x1, blocking collectives, per_device(): block = lax.all_to_all(targets, GZ, split_axis=0, concat_axis=2, tiled=True)  53.7 us
    all_to_all x1, blocking collectives, per_device(): lax.all_to_all(result, 'gy', split_axis=1, concat_axis=2, tiled=True)  52.5 us
    all_to_all x1, blocking collectives, per_device(): block = lax.all_to_all(block, 'gy', split_axis=2, concat_axis=1, tiled=True)  51.5 us
    all_to_all x1, waiting for transfers between devices, per_device(): lax.all_to_all(block, GX_GZ, split_axis=1, concat_axis=0, tiled=True)  46.8 us
    dot_general x1, matrix products, per_device(): result = jnp.einsum('abc,jb->ajc', result, basis_second, precision=high)  14.7 us
    dot_general x2, local copies, waits for them, and re-layouts, per_device(): jnp.dot(block.reshape(-1, full_three), basis_third, precision=high)  10.9 us
  transfers between devices with their start and end apart: 1, of which 1 were waited for; matrix products, arithmetic and copies ran while one was open for 0% of the time, Pallas kernels for 0%

commit v1 on v0

v1 whole, which is shorter than its diff:
```python
import functools

import jax
import jax.numpy as jnp
from jax import lax
from jax.experimental import pallas as pl
from jax.experimental.pallas import tpu as pltpu
from jax.sharding import PartitionSpec as P

MESH = pl.DeviceIdType.MESH
BF = jnp.bfloat16
F32 = jnp.float32
STEPS = 4
DEPTH = 512


def halves(value):
    high = value.astype(BF)
    return high, (value - high.astype(F32)).astype(BF)


def kernel(
    t_ref, b1_ref, b2_ref, b3_ref, e1_ref, e2_ref, e3_ref, noise_ref, o_ref,
    re1, se2, re2, se3, rq1, sq2, rq2, sq3, r3, s3,
    re3p, se2p, re2p, se1p, rq3p, sq2p, rq2p, sq1p,
    b1f, b2f, b3f, b3c, b3tc, b2l, b2tl, b1l, b1tl, lhs, rhs, e1b,
    base_sem, send, in_e1, in_q1, in_e2, in_q2, in_mid, in_e3p, in_q3p, in_e2p, in_q2p, in_out,
):
    w, x, q = lax.axis_index("gx"), lax.axis_index("gy"), lax.axis_index("gz")
    y, z, core = w // 2, (q // 2) * 2 + w % 2, q % 2
    beta = w * 4 + q

    def far(n):
        pair = n // 2
        y2 = (y + pair % 4) % 4
        z2 = (z + pair % 4 + pair // 4) % 4
        c2 = (core + n % 2) % 2
        return y2 * 2 + z2 % 2, (z2 // 2) * 2 + c2

    def push(src, dst, sem, arrival, where):
        pltpu.make_async_remote_copy(
            src_ref=src, dst_ref=dst, send_sem=send.at[sem], recv_sem=arrival,
            device_id=where, device_id_type=MESH,
        ).start()

    def await_bytes(ref, sem):
        pltpu.make_async_copy(ref, ref, sem).wait()

    loads = [
        pltpu.make_async_copy(ref, buf, base_sem.at[n])
        for n, (ref, buf) in enumerate(((b3_ref, b3f), (b2_ref, b2f), (b1_ref, b1f)))
    ]
    for load in loads:
        load.start()

    barrier = pltpu.get_barrier_semaphore()

    def greet(n, _):
        w2, q2 = far(n)
        pl.semaphore_signal(barrier, inc=1, device_id=(w2, x, q2), device_id_type=MESH)
        return _

    for d in (1, 2, 3):
        pl.semaphore_signal(barrier, inc=1, device_id=(w, (x + d) % 4, q), device_id_type=MESH)
    lax.fori_loop(1, 32, greet, 0)
    pl.semaphore_wait(barrier, 34)

    def first(s, _):
        two = pl.ds(s * 2, 2)
        for d in (2, 1, 3):
            q2, x2 = (q + d) % 4, (x + d) % 4
            push(t_ref.at[pl.ds(q2 * 8 + s * 2, 2)], re1.at[q, two], 0, in_e1.at[s], (w, x, q2))
            push(t_ref.at[pl.ds(32 + x2 * 8 + s * 2, 2)], rq1.at[two, x], 1, in_q1.at[s], (w, x2, q))
        pltpu.make_async_copy(t_ref.at[pl.ds(q * 8 + s * 2, 2)], re1.at[q, two], in_e1.at[s]).start()
        pltpu.make_async_copy(t_ref.at[pl.ds(32 + x * 8 + s * 2, 2)], rq1.at[two, x], in_q1.at[s]).start()
        return _

    lax.fori_loop(0, STEPS, first, 0)

    def columns(target, value):
        high, low = halves(value)
        target[0:512, :] = high
        target[512:1024, :] = low
        target[1024:1536, :] = high

    def rows(target, value):
        high, low = halves(value)
        target[:, 0:512] = high
        target[:, 512:1024] = high
        target[:, 1024:1536] = low

    loads[0].wait()
    columns(b3c, b3f[...])
    loads[1].wait()
    rows(b2tl, b2f[...].T)

    def data_left(piece, factor):
        for k in range(4):
            high, low = halves(piece(k))
            lhs[:, k * 128 : k * 128 + 128] = high
            lhs[:, 512 + k * 128 : 640 + k * 128] = high
            lhs[:, 1024 + k * 128 : 1152 + k * 128] = low
        return jnp.dot(lhs[...], factor[...], preferred_element_type=F32)

    def data_right(factor, piece):
        for k in range(2):
            high, low = halves(piece(k))
            lanes = slice(k * 128, k * 128 + 128)
            rhs[0:512, lanes] = high
            rhs[512:1024, lanes] = low
            rhs[1024:1536, lanes] = high
        return jnp.dot(factor[...], rhs[...], preferred_element_type=F32)

    def stage_one(s, _):
        two = pl.ds(s * 2, 2)
        await_bytes(re1.at[:, two], in_e1.at[s])
        out = data_left(lambda k: re1[k, two].reshape(256, 128), b3c)
        for n in range(4):
            se2[n, two] = out[:, n * 128 : n * 128 + 128].reshape(2, 128, 128)
        for d in (2, 1, 3):
            x2 = (x + d) % 4
            push(se2.at[x2, two], re2.at[two, x], 2, in_e2.at[s], (w, x2, q))
        re2[two, x] = se2[x, two]

        await_bytes(rq1.at[two], in_q1.at[s])
        out = data_right(b2tl, lambda k: rq1[s * 2 + k].reshape(512, 128))
        sq2[s * 2] = out[:, 0:128]
        sq2[s * 2 + 1] = out[:, 128:256]

        def spread(n, _):
            w2, q2 = far(n)
            push(
                sq2.at[two, pl.ds((w2 * 4 + q2) * 16, 16)], rq2.at[q, w, two],
                3, in_q2.at[s], (w2, x, q2),
            )
            return _

        lax.fori_loop(1, 32, spread, 0)
        rq2[q, w, two] = sq2[two, pl.ds(pl.multiple_of(beta * 16, 16), 16)]
        return _

    lax.fori_loop(0, STEPS, stage_one, 0)

    loads[2].wait()
    rows(b1tl, b1f[...].T)
    rows(b1l, b1f[...])
    e1b[...] = jnp.broadcast_to(e1_ref[...], (128, DEPTH)).T

    def stage_two(s, _):
        two = pl.ds(s * 2, 2)
        await_bytes(re2.at[two, pl.ds(0, 3)], in_e2.at[s])
        out = data_right(b2tl, lambda k: re2[s * 2 + k].reshape(512, 128))
        se3[s * 2] = out[:, 0:128]
        se3[s * 2 + 1] = out[:, 128:256]

        def spread(n, _):
            w2, q2 = far(n)
            push(
                se3.at[two, pl.ds((w2 * 4 + q2) * 16, 16)], r3.at[w, 0, q, two],
                4, in_mid.at[0], (w2, x, q2),
            )
            return _

        lax.fori_loop(1, 32, spread, 0)
        r3[w, 0, q, two] = se3[two, pl.ds(pl.multiple_of(beta * 16, 16), 16)]

        await_bytes(sq2.at[pl.ds(0, 2), pl.ds(0, 496)], in_q2.at[s])
        out = data_left(lambda k: rq2[k, :, two].reshape(256, 128), b3c)
        for n in range(4):
            sq3[n, :, two] = out[:, n * 128 : n * 128 + 128].reshape(8, 2, 16, 128)
        for d in (2, 1, 3):
            x2 = (x + d) % 4
            push(sq3.at[x2, :, two], r3.at[:, 1, x, two], 5, in_mid.at[1], (w, x2, q))
        r3[:, 1, x, two] = sq3[x, :, two]
        return _

    lax.fori_loop(0, STEPS, stage_two, 0)

    rows(b2l, b2f[...])
    columns(b3tc, b3f[...].T)

    await_bytes(se3.at[:, pl.ds(0, 496)], in_mid.at[0])
    await_bytes(sq3.at[pl.ds(0, 3)], in_mid.at[1])

    flat = r3.reshape(8192, 128)
    along = e3_ref[pl.ds(x, 1), :]

    def middle(t, _):
        for pair in range(2):
            at = t * 4 + pair * 2
            rotated = data_right(b1tl, lambda k: flat[pl.ds(at + k, DEPTH, stride=16), :])
            scaled = []
            for k in range(2):
                spectrum = e1b[...] * e2_ref[beta * 16 + at + k] * along + noise_ref[0]
                scaled.append(rotated[:, k * 128 : k * 128 + 128] / spectrum)
            out = data_right(b1l, lambda k: scaled[k])
            for k in range(2):
                s3[at + k] = out[:, k * 128 : k * 128 + 128].reshape(8, 2, 4, 8, 128)
        four = pl.ds(t * 4, 4)
        for d in (2, 1, 3):
            x2 = (x + d) % 4
            push(s3.at[four, :, 1, x2], rq3p.at[x, four], 6, in_q3p.at[t], (w, x2, q))

        def spread(n, _):
            w2, q2 = far(n)
            push(s3.at[four, w2, 0, q2], re3p.at[beta, four], 7, in_e3p.at[0], (w2, x, q2))
            return _

        lax.fori_loop(1, 32, spread, 0)
        rq3p[x, four] = s3[four, :, 1, x]
        re3p[beta, four] = s3[four, w, 0, q]
        return _

    lax.fori_loop(0, STEPS, middle, 0)

    def back_q3(t, _):
        four = pl.ds(t * 4, 4)
        await_bytes(rq3p.at[pl.ds(0, 3), four], in_q3p.at[t])
        out = data_left(lambda k: rq3p[k, four].reshape(256, 128), b3tc)
        for n in range(4):
            sq2p[n, four] = out[:, n * 128 : n * 128 + 128].reshape(4, 8, 8, 128)

        def spread(n, _):
            w2, q2 = far(n)
            push(sq2p.at[q2, four, w2], rq2p.at[beta, four], 8, in_q2p.at[0], (w2, x, q2))
            return _

        lax.fori_loop(1, 32, spread, 0)
        rq2p[beta, four] = sq2p[q, four, w]
        return _

    lax.fori_loop(0, STEPS, back_q3, 0)

    await_bytes(re3p.at[pl.ds(0, 31)], in_e3p.at[0])
    flat_e = re3p.reshape(4096, 128)

    def back_e3(s, _):
        two = pl.ds(s * 2, 2)
        out = data_right(b2l, lambda k: flat_e[pl.ds(s * 2 + k, DEPTH, stride=8), :])
        for k in range(2):
            se2p[s * 2 + k] = out[:, k * 128 : k * 128 + 128].reshape(4, 128, 128)
        for d in (2, 1, 3):
            x2 = (x + d) % 4
            push(se2p.at[two, x2], re2p.at[x, two], 9, in_e2p.at[s], (w, x2, q))
        re2p[x, two] = se2p[two, x]
        return _

    lax.fori_loop(0, STEPS, back_e3, 0)

    def back_e2(s, _):
        two = pl.ds(s * 2, 2)
        await_bytes(re2p.at[pl.ds(0, 3), two], in_e2p.at[s])
        out = data_left(lambda k: re2p[k, two].reshape(256, 128), b3tc)
        for n in range(4):
            se1p[n, two] = out[:, n * 128 : n * 128 + 128].reshape(2, 128, 128)
        here = o_ref.at[pl.ds(q * 8 + s * 2, 2)]
        for d in (2, 1, 3):
            q2 = (q + d) % 4
            push(se1p.at[q2, two], here, 10, in_out.at[0], (w, x, q2))
        pltpu.make_async_copy(se1p.at[q, two], here, in_out.at[0]).start()
        return _

    lax.fori_loop(0, STEPS, back_e2, 0)

    await_bytes(rq2p.at[pl.ds(0, 31)], in_q2p.at[0])
    flat_q = rq2p.reshape(4096, 128)

    def back_q2(s, _):
        two = pl.ds(s * 2, 2)
        out = data_right(b2l, lambda k: flat_q[pl.ds(s * 2 + k, DEPTH, stride=8), :])
        for k in range(2):
            sq1p[s * 2 + k] = out[:, k * 128 : k * 128 + 128].reshape(4, 128, 128)
        here = o_ref.at[pl.ds(32 + x * 8 + s * 2, 2)]
        for d in (2, 1, 3):
            x2 = (x + d) % 4
            push(sq1p.at[two, x2], here, 11, in_out.at[1], (w, x2, q))
        pltpu.make_async_copy(sq1p.at[two, x], here, in_out.at[1]).start()
        return _

    lax.fori_loop(0, STEPS, back_q2, 0)

    await_bytes(re1, in_out.at[0])
    await_bytes(re1, in_out.at[1])
    for sem in (0, 1, 2, 5, 6, 9, 10, 11):
        await_bytes(re1.at[pl.ds(0, 3)], send.at[sem])
    for sem in (3, 4, 7, 8):
        await_bytes(rq2p.at[pl.ds(0, 31)], send.at[sem])


def per_device(targets, basis_first, basis_second, basis_third, eigen_first, eigen_second, eigen_third, noise):
    half = [
        (4, 8, 128, 128), (4, 8, 128, 128), (8, 4, 128, 128), (8, 512, 128),
        (8, 4, 128, 128), (8, 512, 128), (4, 8, 8, 16, 128), (4, 8, 8, 16, 128),
        (8, 2, 4, 8, 16, 128), (16, 8, 2, 4, 8, 128),
        (32, 16, 8, 128), (8, 4, 128, 128), (4, 8, 128, 128), (4, 8, 128, 128),
        (4, 16, 8, 8, 128), (4, 16, 8, 8, 128), (32, 16, 8, 128), (8, 4, 128, 128),
    ]
    scratch = [pltpu.VMEM(shape, F32) for shape in half]
    scratch += [pltpu.VMEM((512, 512), F32)] * 3
    scratch += [pltpu.VMEM((1536, 512), BF)] * 2 + [pltpu.VMEM((512, 1536), BF)] * 4
    scratch += [pltpu.VMEM((256, 1536), BF), pltpu.VMEM((1536, 256), BF), pltpu.VMEM((512, 128), F32)]
    dma = pltpu.SemaphoreType.DMA
    scratch += [dma((3,)), dma((12,))] + [dma((STEPS,))] * 4
    scratch += [dma((2,)), dma((1,)), dma((STEPS,)), dma((STEPS,)), dma((1,)), dma((2,))]
    whole = pl.BlockSpec(memory_space=pl.ANY)
    vmem = pl.BlockSpec(memory_space=pltpu.VMEM)
    smem = pl.BlockSpec(memory_space=pltpu.SMEM)
    return pl.pallas_call(
        kernel,
        out_shape=jax.ShapeDtypeStruct((64, 128, 128), F32),
        in_specs=[whole, whole, whole, whole, vmem, smem, vmem, smem],
        out_specs=whole,
        scratch_shapes=scratch,
        compiler_params=pltpu.CompilerParams(
            collective_id=0, has_side_effects=True, vmem_limit_bytes=67043328
        ),
        name="kron_solve",
    )(
        targets, basis_first, basis_second, basis_third,
        eigen_first.reshape(1, 512), eigen_second, eigen_third.reshape(4, 128), noise,
    )


def solution(mesh):
    in_specs = (P("gx", "gy", "gz"), P(), P(), P(), P(), P(), P(), P())
    return jax.shard_map(
        per_device, mesh=mesh, in_specs=in_specs, out_specs=P("gx", "gy", "gz"), check_vma=False
    )
```

time: 465 us -> 188 us (0.40); the launches traced: 456 us -> 188 us
  blocking collectives: 278 us -> 0 us
  Pallas kernels: 0 us -> 182 us
  matrix products: 59.5 us -> 0 us
  local copies, waits for them, and re-layouts: 61.7 us -> 4.7 us
  waiting for transfers between devices: 46.8 us -> 0 us
  starting transfers between devices: 8.96 us -> 0 us
    all_to_all x6 -> x0, blocking collectives: 278 us -> none  [the longest x1 61.1 us: per_device(): lax.all_to_all(result, GX_GZ, split_axis=0, concat_axis=1, tiled=True)]
    pallas_call x0 -> x1, Pallas kernels: none -> 182 us  [per_device(): pl.pallas_call(kernel, out_shape=jax.ShapeDtypeStruct((64, 128, 128), F32...]
    dot_general x6 -> x0, matrix products: 59.5 us -> none  [the longest x1 14.7 us: per_device(): result = jnp.einsum('abc,jb->ajc', result, basis_second, precision=high)]
    all_to_all x1 -> x0, waiting for transfers between devices: 46.8 us -> none  [per_device(): lax.all_to_all(block, GX_GZ, split_axis=1, concat_axis=0, tiled=True)]
    all_to_all x8 -> x0, local copies, waits for them, and re-layouts: 27 us -> none  [the longest x2 10.3 us: per_device(): block = lax.all_to_all(block, 'gy', split_axis=2, concat_axis=1, tiled=True)]
    dot_general x3 -> x0, local copies, waits for them, and re-layouts: 16.4 us -> none  [the longest x2 10.9 us: per_device(): jnp.dot(block.reshape(-1, full_three), basis_third, precision=high)]
    transpose x2 -> x0, local copies, waits for them, and re-layouts: 10.9 us -> none  [the longest x1 5.47 us: per_device(): block = jnp.einsum('ajc,jb->abc', block, basis_second, precision=high)]
    all_to_all x1 -> x0, starting transfers between devices: 8.96 us -> none  [per_device(): lax.all_to_all(block, GX_GZ, split_axis=1, concat_axis=0, tiled=True)]
  transfers between devices with their start and end apart: 1 -> 0, of which waited for: 1 -> 0; matrix products, arithmetic and copies ran while one was open for 0% -> 0% of each run, Pallas kernels for 0% -> 0%
where the time goes in v1:
time: 188 us
  Pallas kernels  182 us (97%)
  local copies, waits for them, and re-layouts  4.7 us (2%)
    pallas_call x1, Pallas kernels, per_device(): pl.pallas_call(kernel, out_shape=jax.ShapeDtypeStruct((64, 128, 128), F32...  182 us
    unnamed x1, local copies, waits for them, and re-layouts  4.7 us

profile of v1, /device:TPU:33, one launch (start us, length us, event | category | flops | bytes accessed | tf_op | source)
XLA Modules:
  0.0 187.5 jit_solution(1550344462108866983)
XLA Ops:
  0.7 182.2 %kron_solve.1 = f32[64,128,128]{2,1,0:T(8,128)} custom-call(f32[64,128,128]{2,1,0:T(8,128)} %t_ref.1, f32[512,512]{1,0:T(8,128)} %b1_ref.1, f32[512,512]{1,0:T(8,128)} %b2_ref.1, f32[512,512]{1,0:T(8,128)} %b3_ref.1, f32[1,512]{1,0:T(1,128)} %bitcast.2, f32[512]{0:T(512)} %e2_ref.1, f32[4,128]{1,0:T(4,128)} %bitcast.3, f32[1]{0:T(128)S(6)} %copy.10.noise_ref), custom_call_target="tpu_custom_call" | custom-call | tf_op jit(solution)/shard_map/kron_solve/pallas_call | solution.py:308
  182.8 4.7 %copy.11 = f32[64,128,128]{2,1,0:T(8,128)} copy(f32[64,128,128]{2,1,0:T(8,128)} %kron_solve.1) | data formatting | bytes 8388608

commit v2 on v1

--- a/solution.py
+++ b/solution.py
@@ -23,7 +23,7 @@
     t_ref, b1_ref, b2_ref, b3_ref, e1_ref, e2_ref, e3_ref, noise_ref, o_ref,
     re1, se2, re2, se3, rq1, sq2, rq2, sq3, r3, s3,
     re3p, se2p, re2p, se1p, rq3p, sq2p, rq2p, sq1p,
-    b1f, b2f, b3f, b3c, b3tc, b2l, b2tl, b1l, b1tl, lhs, rhs, e1b,
+    b1f, b2f, b3f, b3c, b3tc, b2l, b2tl, b1l, b1tl, lhs, rhs, mid, e1b,
     base_sem, send, in_e1, in_q1, in_e2, in_q2, in_mid, in_e3p, in_q3p, in_e2p, in_q2p, in_out,
 ):
     w, x, q = lax.axis_index("gx"), lax.axis_index("gy"), lax.axis_index("gz")
@@ -143,7 +143,15 @@
 
     loads[2].wait()
     rows(b1tl, b1f[...].T)
-    rows(b1l, b1f[...])
+    place = lax.broadcasted_iota(jnp.int32, (DEPTH, DEPTH), 0)
+    source = (place % 128) // 2 * 8 + place // 128 * 2 + place % 2
+    pick = (lax.broadcasted_iota(jnp.int32, (DEPTH, DEPTH), 1) == source).astype(F32).astype(BF)
+    high, low = halves(b1f[...])
+    high = jnp.dot(pick, high, preferred_element_type=F32).astype(BF)
+    low = jnp.dot(pick, low, preferred_element_type=F32).astype(BF)
+    b1l[:, 0:512] = high
+    b1l[:, 512:1024] = high
+    b1l[:, 1024:1536] = low
     e1b[...] = jnp.broadcast_to(e1_ref[...], (128, DEPTH)).T
 
     def stage_two(s, _):
@@ -183,71 +191,81 @@
     await_bytes(sq3.at[pl.ds(0, 3)], in_mid.at[1])
 
     flat = r3.reshape(8192, 128)
+    flat_s = s3.reshape(8192, 128)
     along = e3_ref[pl.ds(x, 1), :]
 
-    def middle(t, _):
-        for pair in range(2):
-            at = t * 4 + pair * 2
-            rotated = data_right(b1tl, lambda k: flat[pl.ds(at + k, DEPTH, stride=16), :])
-            scaled = []
+    def middle(pair, _):
+        at = pair * 2
+        rotated = data_right(b1tl, lambda k: flat[pl.ds(at + k, DEPTH, stride=16), :])
+        for k in range(2):
+            lanes = slice(k * 128, k * 128 + 128)
+            spectrum = e1b[...] * e2_ref[beta * 16 + at + k] * along + noise_ref[0]
+            high, low = halves(rotated[:, lanes] / spectrum)
+            mid[pair, 0:512, lanes] = high
+            mid[pair, 512:1024, lanes] = low
+            mid[pair, 1024:1536, lanes] = high
+        return _
+
+    lax.fori_loop(0, 8, middle, 0)
+
+    def back_mid(s, _):
+        factor = b1l[pl.ds(pl.multiple_of(s * 128, 128), 128), :]
+        for pair in range(8):
+            out = jnp.dot(factor, mid[pair], preferred_element_type=F32)
             for k in range(2):
-                spectrum = e1b[...] * e2_ref[beta * 16 + at + k] * along + noise_ref[0]
-                scaled.append(rotated[:, k * 128 : k * 128 + 128] / spectrum)
-            out = data_right(b1l, lambda k: scaled[k])
-            for k in range(2):
-                s3[at + k] = out[:, k * 128 : k * 128 + 128].reshape(8, 2, 4, 8, 128)
-        four = pl.ds(t * 4, 4)
-        for d in (2, 1, 3):
-            x2 = (x + d) % 4
-            push(s3.at[four, :, 1, x2], rq3p.at[x, four], 6, in_q3p.at[t], (w, x2, q))
+                flat_s[pl.ds(s * 2048 + pair * 2 + k, 128, stride=16), :] = out[:, k * 128 : k * 128 + 128]
+        for d in (2, 1, 3):
+            x2 = (x + d) % 4
+            push(s3.at[s, :, 1, x2], rq3p.at[x, s], 6, in_q3p.at[s], (w, x2, q))
 
         def spread(n, _):
             w2, q2 = far(n)
-            push(s3.at[four, w2, 0, q2], re3p.at[beta, four], 7, in_e3p.at[0], (w2, x, q2))
+            push(
+                s3.at[s, w2, 0, q2],
+                re3p.at[pl.ds(s * 2, 2), pl.ds(pl.multiple_of(beta * 16, 16), 16)],
+                7, in_e3p.at[s], (w2, x, q2),
+            )
             return _
 
         lax.fori_loop(1, 32, spread, 0)
-        rq3p[x, four] = s3[four, :, 1, x]
-        re3p[beta, four] = s3[four, w, 0, q]
-        return _
-
-    lax.fori_loop(0, STEPS, middle, 0)
-
-    def back_q3(t, _):
-        four = pl.ds(t * 4, 4)
-        await_bytes(rq3p.at[pl.ds(0, 3), four], in_q3p.at[t])
-        out = data_left(lambda k: rq3p[k, four].reshape(256, 128), b3tc)
+        rq3p[x, s] = s3[s, :, 1, x]
+        re3p[pl.ds(s * 2, 2), pl.ds(pl.multiple_of(beta * 16, 16), 16)] = s3[s, w, 0, q]
+        return _
+
+    lax.fori_loop(0, STEPS, back_mid, 0)
+
+    def back_one(s, _):
+        two = pl.ds(s * 2, 2)
+        await_bytes(se3.at[pl.ds(0, 2), pl.ds(0, 496)], in_e3p.at[s])
+        out = data_right(b2l, lambda k: re3p[s * 2 + k])
+        for k in range(2):
+            se2p[s * 2 + k] = out[:, k * 128 : k * 128 + 128].reshape(4, 128, 128)
+        for d in (2, 1, 3):
+            x2 = (x + d) % 4
+            push(se2p.at[two, x2], re2p.at[x, two], 9, in_e2p.at[s], (w, x2, q))
+        re2p[x, two] = se2p[two, x]
+
+        await_bytes(rq3p.at[pl.ds(0, 3), s], in_q3p.at[s])
+        out = data_left(lambda k: rq3p[k, s].reshape(256, 128), b3tc)
         for n in range(4):
-            sq2p[n, four] = out[:, n * 128 : n * 128 + 128].reshape(4, 8, 8, 128)
+            sq2p[n, s] = out[:, n * 128 : n * 128 + 128].reshape(8, 2, 16, 128)
 
         def spread(n, _):
             w2, q2 = far(n)
-            push(sq2p.at[q2, four, w2], rq2p.at[beta, four], 8, in_q2p.at[0], (w2, x, q2))
+            push(
+                sq2p.at[q2, s, w2],
+                rq2p.at[two, pl.ds(pl.multiple_of(beta * 16, 16), 16)],
+                8, in_q2p.at[s], (w2, x, q2),
+            )
             return _
 
         lax.fori_loop(1, 32, spread, 0)
-        rq2p[beta, four] = sq2p[q, four, w]
-        return _
-
-    lax.fori_loop(0, STEPS, back_q3, 0)
-
-    await_bytes(re3p.at[pl.ds(0, 31)], in_e3p.at[0])
-    flat_e = re3p.reshape(4096, 128)
-
-    def back_e3(s, _):
-        two = pl.ds(s * 2, 2)
-        out = data_right(b2l, lambda k: flat_e[pl.ds(s * 2 + k, DEPTH, stride=8), :])
-        for k in range(2):
-            se2p[s * 2 + k] = out[:, k * 128 : k * 128 + 128].reshape(4, 128, 128)
-        for d in (2, 1, 3):
-            x2 = (x + d) % 4
-            push(se2p.at[two, x2], re2p.at[x, two], 9, in_e2p.at[s], (w, x2, q))
-        re2p[x, two] = se2p[two, x]
-        return _
-
-    lax.fori_loop(0, STEPS, back_e3, 0)
-
-    def back_e2(s, _):
+        rq2p[two, pl.ds(pl.multiple_of(beta * 16, 16), 16)] = sq2p[q, s, w]
+        return _
+
+    lax.fori_loop(0, STEPS, back_one, 0)
+
+    def back_two(s, _):
         two = pl.ds(s * 2, 2)
         await_bytes(re2p.at[pl.ds(0, 3), two], in_e2p.at[s])
         out = data_left(lambda k: re2p[k, two].reshape(256, 128), b3tc)
@@ -258,16 +276,9 @@
             q2 = (q + d) % 4
             push(se1p.at[q2, two], here, 10, in_out.at[0], (w, x, q2))
         pltpu.make_async_copy(se1p.at[q, two], here, in_out.at[0]).start()
-        return _
-
-    lax.fori_loop(0, STEPS, back_e2, 0)
-
-    await_bytes(rq2p.at[pl.ds(0, 31)], in_q2p.at[0])
-    flat_q = rq2p.reshape(4096, 128)
-
-    def back_q2(s, _):
-        two = pl.ds(s * 2, 2)
-        out = data_right(b2l, lambda k: flat_q[pl.ds(s * 2 + k, DEPTH, stride=8), :])
+
+        await_bytes(se3.at[pl.ds(0, 2), pl.ds(0, 496)], in_q2p.at[s])
+        out = data_right(b2l, lambda k: rq2p[s * 2 + k])
         for k in range(2):
             sq1p[s * 2 + k] = out[:, k * 128 : k * 128 + 128].reshape(4, 128, 128)
         here = o_ref.at[pl.ds(32 + x * 8 + s * 2, 2)]
@@ -277,31 +288,32 @@
         pltpu.make_async_copy(sq1p.at[two, x], here, in_out.at[1]).start()
         return _
 
-    lax.fori_loop(0, STEPS, back_q2, 0)
+    lax.fori_loop(0, STEPS, back_two, 0)
 
     await_bytes(re1, in_out.at[0])
     await_bytes(re1, in_out.at[1])
     for sem in (0, 1, 2, 5, 6, 9, 10, 11):
         await_bytes(re1.at[pl.ds(0, 3)], send.at[sem])
     for sem in (3, 4, 7, 8):
-        await_bytes(rq2p.at[pl.ds(0, 31)], send.at[sem])
+        await_bytes(se3.at[:, pl.ds(0, 496)], send.at[sem])
 
 
 def per_device(targets, basis_first, basis_second, basis_third, eigen_first, eigen_second, eigen_third, noise):
     half = [
         (4, 8, 128, 128), (4, 8, 128, 128), (8, 4, 128, 128), (8, 512, 128),
         (8, 4, 128, 128), (8, 512, 128), (4, 8, 8, 16, 128), (4, 8, 8, 16, 128),
-        (8, 2, 4, 8, 16, 128), (16, 8, 2, 4, 8, 128),
-        (32, 16, 8, 128), (8, 4, 128, 128), (4, 8, 128, 128), (4, 8, 128, 128),
-        (4, 16, 8, 8, 128), (4, 16, 8, 8, 128), (32, 16, 8, 128), (8, 4, 128, 128),
+        (8, 2, 4, 8, 16, 128), (4, 8, 2, 4, 2, 16, 128),
+        (8, 512, 128), (8, 4, 128, 128), (4, 8, 128, 128), (4, 8, 128, 128),
+        (4, 4, 8, 2, 16, 128), (4, 4, 8, 2, 16, 128), (8, 512, 128), (8, 4, 128, 128),
     ]
     scratch = [pltpu.VMEM(shape, F32) for shape in half]
     scratch += [pltpu.VMEM((512, 512), F32)] * 3
     scratch += [pltpu.VMEM((1536, 512), BF)] * 2 + [pltpu.VMEM((512, 1536), BF)] * 4
-    scratch += [pltpu.VMEM((256, 1536), BF), pltpu.VMEM((1536, 256), BF), pltpu.VMEM((512, 128), F32)]
+    scratch += [pltpu.VMEM((256, 1536), BF), pltpu.VMEM((1536, 256), BF)]
+    scratch += [pltpu.VMEM((8, 1536, 256), BF), pltpu.VMEM((512, 128), F32)]
     dma = pltpu.SemaphoreType.DMA
     scratch += [dma((3,)), dma((12,))] + [dma((STEPS,))] * 4
-    scratch += [dma((2,)), dma((1,)), dma((STEPS,)), dma((STEPS,)), dma((1,)), dma((2,))]
+    scratch += [dma((2,))] + [dma((STEPS,))] * 4 + [dma((2,))]
     whole = pl.BlockSpec(memory_space=pl.ANY)
     vmem = pl.BlockSpec(memory_space=pltpu.VMEM)
     smem = pl.BlockSpec(memory_space=pltpu.SMEM)

time: 188 us -> 177 us (0.941)
  Pallas kernels: 182 us -> 171 us
    pallas_call x1, Pallas kernels: 182 us -> 171 us  [per_device(): pl.pallas_call(kernel, out_shape=jax.ShapeDtypeStruct((64, 128, 128), F32...]
where the time goes in v2:
time: 177 us; the launch traced here: 176 us
  Pallas kernels  171 us (97%)
  local copies, waits for them, and re-layouts  4.7 us (3%)
    pallas_call x1, Pallas kernels, per_device(): pl.pallas_call(kernel, out_shape=jax.ShapeDtypeStruct((64, 128, 128), F32...  171 us
    unnamed x1, local copies, waits for them, and re-layouts  4.7 us

profile of v2, /device:TPU:33, one launch (start us, length us, event | category | flops | bytes accessed | tf_op | source)
XLA Modules:
  0.0 176.5 jit_solution(6412598669562765422)
XLA Ops:
  0.7 171.1 %kron_solve.1 = f32[64,128,128]{2,1,0:T(8,128)} custom-call(f32[64,128,128]{2,1,0:T(8,128)} %t_ref.1, f32[512,512]{1,0:T(8,128)} %b1_ref.1, f32[512,512]{1,0:T(8,128)} %b2_ref.1, f32[512,512]{1,0:T(8,128)} %b3_ref.1, f32[1,512]{1,0:T(1,128)} %bitcast.2, f32[512]{0:T(512)} %e2_ref.1, f32[4,128]{1,0:T(4,128)} %bitcast.3, f32[1]{0:T(128)S(6)} %copy.10.noise_ref), custom_call_target="tpu_custom_call" | custom-call | tf_op jit(solution)/shard_map/kron_solve/pallas_call | solution.py:320
  171.8 4.7 %copy.11 = f32[64,128,128]{2,1,0:T(8,128)} copy(f32[64,128,128]{2,1,0:T(8,128)} %kron_solve.1) | data formatting | bytes 8388608

commit v3 on v2

--- a/solution.py
+++ b/solution.py
@@ -12,6 +12,7 @@
 F32 = jnp.float32
 STEPS = 4
 DEPTH = 512
+ORDER = ("qe", "eq", "eq", "eq")
 
 
 def halves(value):
@@ -30,12 +31,28 @@
     y, z, core = w // 2, (q // 2) * 2 + w % 2, q % 2
     beta = w * 4 + q
 
-    def far(n):
-        pair = n // 2
-        y2 = (y + pair % 4) % 4
-        z2 = (z + pair % 4 + pair // 4) % 4
-        c2 = (core + n % 2) % 2
+    def far(dy, dz, dc):
+        y2, z2, c2 = (y + dy) % 4, (z + dz) % 4, (core + dc) % 2
         return y2 * 2 + z2 % 2, (z2 // 2) * 2 + c2
+
+    def each_far(act):
+        def both(n, _):
+            k = n // 2
+            act(*far(k % 3 + 1, (k % 3 + k // 3) % 3 + 1, n % 2))
+            return _
+
+        def one(n, _):
+            act(*far(n // 2 + 1, 0, n % 2))
+            return _
+
+        def other(n, _):
+            act(*far(0, n // 2 + 1, n % 2))
+            return _
+
+        lax.fori_loop(0, 18, both, 0)
+        lax.fori_loop(0, 6, one, 0)
+        lax.fori_loop(0, 6, other, 0)
+        act(*far(0, 0, 1))
 
     def push(src, dst, sem, arrival, where):
         pltpu.make_async_remote_copy(
@@ -45,6 +62,14 @@
 
     def await_bytes(ref, sem):
         pltpu.make_async_copy(ref, ref, sem).wait()
+
+    def staged(part_e, part_q, order):
+        def body(s, _):
+            for part in order:
+                (part_e if part == "e" else part_q)(s)
+            return _
+
+        lax.fori_loop(0, STEPS, body, 0)
 
     loads = [
         pltpu.make_async_copy(ref, buf, base_sem.at[n])
@@ -55,14 +80,12 @@
 
     barrier = pltpu.get_barrier_semaphore()
 
-    def greet(n, _):
-        w2, q2 = far(n)
+    def greet(w2, q2):
         pl.semaphore_signal(barrier, inc=1, device_id=(w2, x, q2), device_id_type=MESH)
-        return _
 
     for d in (1, 2, 3):
         pl.semaphore_signal(barrier, inc=1, device_id=(w, (x + d) % 4, q), device_id_type=MESH)
-    lax.fori_loop(1, 32, greet, 0)
+    each_far(greet)
     pl.semaphore_wait(barrier, 34)
 
     def first(s, _):
@@ -111,7 +134,7 @@
             rhs[1024:1536, lanes] = high
         return jnp.dot(factor[...], rhs[...], preferred_element_type=F32)
 
-    def stage_one(s, _):
+    def stage_one_e(s):
         two = pl.ds(s * 2, 2)
         await_bytes(re1.at[:, two], in_e1.at[s])
         out = data_left(lambda k: re1[k, two].reshape(256, 128), b3c)
@@ -122,24 +145,23 @@
             push(se2.at[x2, two], re2.at[two, x], 2, in_e2.at[s], (w, x2, q))
         re2[two, x] = se2[x, two]
 
+    def stage_one_q(s):
+        two = pl.ds(s * 2, 2)
         await_bytes(rq1.at[two], in_q1.at[s])
         out = data_right(b2tl, lambda k: rq1[s * 2 + k].reshape(512, 128))
         sq2[s * 2] = out[:, 0:128]
         sq2[s * 2 + 1] = out[:, 128:256]
 
-        def spread(n, _):
-            w2, q2 = far(n)
+        def spread(w2, q2):
             push(
                 sq2.at[two, pl.ds((w2 * 4 + q2) * 16, 16)], rq2.at[q, w, two],
                 3, in_q2.at[s], (w2, x, q2),
             )
-            return _
-
-        lax.fori_loop(1, 32, spread, 0)
+
+        each_far(spread)
         rq2[q, w, two] = sq2[two, pl.ds(pl.multiple_of(beta * 16, 16), 16)]
-        return _
-
-    lax.fori_loop(0, STEPS, stage_one, 0)
+
+    staged(stage_one_e, stage_one_q, ORDER[0])
 
     loads[2].wait()
     rows(b1tl, b1f[...].T)
@@ -154,24 +176,24 @@
     b1l[:, 1024:1536] = low
     e1b[...] = jnp.broadcast_to(e1_ref[...], (128, DEPTH)).T
 
-    def stage_two(s, _):
+    def stage_two_e(s):
         two = pl.ds(s * 2, 2)
         await_bytes(re2.at[two, pl.ds(0, 3)], in_e2.at[s])
         out = data_right(b2tl, lambda k: re2[s * 2 + k].reshape(512, 128))
         se3[s * 2] = out[:, 0:128]
         se3[s * 2 + 1] = out[:, 128:256]
 
-        def spread(n, _):
-            w2, q2 = far(n)
+        def spread(w2, q2):
             push(
                 se3.at[two, pl.ds((w2 * 4 + q2) * 16, 16)], r3.at[w, 0, q, two],
                 4, in_mid.at[0], (w2, x, q2),
             )
-            return _
-
-        lax.fori_loop(1, 32, spread, 0)
+
+        each_far(spread)
         r3[w, 0, q, two] = se3[two, pl.ds(pl.multiple_of(beta * 16, 16), 16)]
 
+    def stage_two_q(s):
+        two = pl.ds(s * 2, 2)
         await_bytes(sq2.at[pl.ds(0, 2), pl.ds(0, 496)], in_q2.at[s])
         out = data_left(lambda k: rq2[k, :, two].reshape(256, 128), b3c)
         for n in range(4):
@@ -180,9 +202,8 @@
             x2 = (x + d) % 4
             push(sq3.at[x2, :, two], r3.at[:, 1, x, two], 5, in_mid.at[1], (w, x2, q))
         r3[:, 1, x, two] = sq3[x, :, two]
-        return _
-
-    lax.fori_loop(0, STEPS, stage_two, 0)
+
+    staged(stage_two_e, stage_two_q, ORDER[1])
 
     rows(b2l, b2f[...])
     columns(b3tc, b3f[...].T)
@@ -218,23 +239,21 @@
             x2 = (x + d) % 4
             push(s3.at[s, :, 1, x2], rq3p.at[x, s], 6, in_q3p.at[s], (w, x2, q))
 
-        def spread(n, _):
-            w2, q2 = far(n)
+        def spread(w2, q2):
             push(
                 s3.at[s, w2, 0, q2],
                 re3p.at[pl.ds(s * 2, 2), pl.ds(pl.multiple_of(beta * 16, 16), 16)],
                 7, in_e3p.at[s], (w2, x, q2),
             )
-            return _
-
-        lax.fori_loop(1, 32, spread, 0)
+
+        each_far(spread)
         rq3p[x, s] = s3[s, :, 1, x]
         re3p[pl.ds(s * 2, 2), pl.ds(pl.multiple_of(beta * 16, 16), 16)] = s3[s, w, 0, q]
         return _
 
     lax.fori_loop(0, STEPS, back_mid, 0)
 
-    def back_one(s, _):
+    def back_one_e(s):
         two = pl.ds(s * 2, 2)
         await_bytes(se3.at[pl.ds(0, 2), pl.ds(0, 496)], in_e3p.at[s])
         out = data_right(b2l, lambda k: re3p[s * 2 + k])
@@ -245,27 +264,26 @@
             push(se2p.at[two, x2], re2p.at[x, two], 9, in_e2p.at[s], (w, x2, q))
         re2p[x, two] = se2p[two, x]
 
+    def back_one_q(s):
+        two = pl.ds(s * 2, 2)
         await_bytes(rq3p.at[pl.ds(0, 3), s], in_q3p.at[s])
         out = data_left(lambda k: rq3p[k, s].reshape(256, 128), b3tc)
         for n in range(4):
             sq2p[n, s] = out[:, n * 128 : n * 128 + 128].reshape(8, 2, 16, 128)
 
-        def spread(n, _):
-            w2, q2 = far(n)
+        def spread(w2, q2):
             push(
                 sq2p.at[q2, s, w2],
                 rq2p.at[two, pl.ds(pl.multiple_of(beta * 16, 16), 16)],
                 8, in_q2p.at[s], (w2, x, q2),
             )
-            return _
-
-        lax.fori_loop(1, 32, spread, 0)
+
+        each_far(spread)
         rq2p[two, pl.ds(pl.multiple_of(beta * 16, 16), 16)] = sq2p[q, s, w]
-        return _
-
-    lax.fori_loop(0, STEPS, back_one, 0)
-
-    def back_two(s, _):
+
+    staged(back_one_e, back_one_q, ORDER[2])
+
+    def back_two_e(s):
         two = pl.ds(s * 2, 2)
         await_bytes(re2p.at[pl.ds(0, 3), two], in_e2p.at[s])
         out = data_left(lambda k: re2p[k, two].reshape(256, 128), b3tc)
@@ -277,6 +295,8 @@
             push(se1p.at[q2, two], here, 10, in_out.at[0], (w, x, q2))
         pltpu.make_async_copy(se1p.at[q, two], here, in_out.at[0]).start()
 
+    def back_two_q(s):
+        two = pl.ds(s * 2, 2)
         await_bytes(se3.at[pl.ds(0, 2), pl.ds(0, 496)], in_q2p.at[s])
         out = data_right(b2l, lambda k: rq2p[s * 2 + k])
         for k in range(2):
@@ -286,9 +306,8 @@
             x2 = (x + d) % 4
             push(sq1p.at[two, x2], here, 11, in_out.at[1], (w, x2, q))
         pltpu.make_async_copy(sq1p.at[two, x], here, in_out.at[1]).start()
-        return _
-
-    lax.fori_loop(0, STEPS, back_two, 0)
+
+    staged(back_two_e, back_two_q, ORDER[3])
 
     await_bytes(re1, in_out.at[0])
     await_bytes(re1, in_out.at[1])

time: 177 us -> 174 us (0.983)
  the two profiles are of different devices: /device:TPU:33 before, /device:TPU:22 now
where the time goes in v3:
time: 174 us
  Pallas kernels  168 us (97%)
  local copies, waits for them, and re-layouts  4.7 us (3%)
    pallas_call x1, Pallas kernels, per_device(): pl.pallas_call(kernel, out_shape=jax.ShapeDtypeStruct((64, 128, 128), F32...  168 us
    unnamed x1, local copies, waits for them, and re-layouts  4.7 us

profile of v3, /device:TPU:22, one launch (start us, length us, event | category | flops | bytes accessed | tf_op | source)
XLA Modules:
  0.0 173.8 jit_solution(16706320490453906274)
XLA Ops:
  0.7 168.4 %kron_solve.1 = f32[64,128,128]{2,1,0:T(8,128)} custom-call(f32[64,128,128]{2,1,0:T(8,128)} %t_ref.1, f32[512,512]{1,0:T(8,128)} %b1_ref.1, f32[512,512]{1,0:T(8,128)} %b2_ref.1, f32[512,512]{1,0:T(8,128)} %b3_ref.1, f32[1,512]{1,0:T(1,128)} %bitcast.2, f32[512]{0:T(512)} %e2_ref.1, f32[4,128]{1,0:T(4,128)} %bitcast.3, f32[1]{0:T(128)S(6)} %copy.10.noise_ref), custom_call_target="tpu_custom_call" | custom-call | tf_op jit(solution)/shard_map/kron_solve/pallas_call | solution.py:339
  169.1 4.7 %copy.11 = f32[64,128,128]{2,1,0:T(8,128)} copy(f32[64,128,128]{2,1,0:T(8,128)} %kron_solve.1) | data formatting | bytes 8388608

commit v4 on v3

--- a/solution.py
+++ b/solution.py
@@ -24,8 +24,8 @@
     t_ref, b1_ref, b2_ref, b3_ref, e1_ref, e2_ref, e3_ref, noise_ref, o_ref,
     re1, se2, re2, se3, rq1, sq2, rq2, sq3, r3, s3,
     re3p, se2p, re2p, se1p, rq3p, sq2p, rq2p, sq1p,
-    b1f, b2f, b3f, b3c, b3tc, b2l, b2tl, b1l, b1tl, lhs, rhs, mid, e1b,
-    base_sem, send, in_e1, in_q1, in_e2, in_q2, in_mid, in_e3p, in_q3p, in_e2p, in_q2p, in_out,
+    b1f, b2f, b3f, b3c, b3tc, b2l, b2tl, b1l, b1tm, lhs, rhs, mid, e1b,
+    base_sem, send, in_e1, in_q1, in_e2, in_q2, in_me, in_mq, in_e3p, in_q3p, in_e2p, in_q2p, in_out,
 ):
     w, x, q = lax.axis_index("gx"), lax.axis_index("gy"), lax.axis_index("gz")
     y, z, core = w // 2, (q // 2) * 2 + w % 2, q % 2
@@ -164,16 +164,21 @@
     staged(stage_one_e, stage_one_q, ORDER[0])
 
     loads[2].wait()
-    rows(b1tl, b1f[...].T)
     place = lax.broadcasted_iota(jnp.int32, (DEPTH, DEPTH), 0)
     source = (place % 128) // 2 * 8 + place // 128 * 2 + place % 2
     pick = (lax.broadcasted_iota(jnp.int32, (DEPTH, DEPTH), 1) == source).astype(F32).astype(BF)
     high, low = halves(b1f[...])
-    high = jnp.dot(pick, high, preferred_element_type=F32).astype(BF)
-    low = jnp.dot(pick, low, preferred_element_type=F32).astype(BF)
-    b1l[:, 0:512] = high
-    b1l[:, 512:1024] = high
-    b1l[:, 1024:1536] = low
+    high = jnp.dot(pick, high, preferred_element_type=F32)
+    low = jnp.dot(pick, low, preferred_element_type=F32)
+    b1l[:, 0:512] = high.astype(BF)
+    b1l[:, 512:1024] = high.astype(BF)
+    b1l[:, 1024:1536] = low.astype(BF)
+    high, low = high.T.astype(BF), low.T.astype(BF)
+    for n in range(STEPS):
+        b1tm[n, :, 0:128] = high[:, n * 128 : n * 128 + 128]
+        b1tm[n, :, 128:256] = high[:, n * 128 : n * 128 + 128]
+        b1tm[n, :, 256:384] = low[:, n * 128 : n * 128 + 128]
+    s3[...] = jnp.zeros_like(s3)
     e1b[...] = jnp.broadcast_to(e1_ref[...], (128, DEPTH)).T
 
     def stage_two_e(s):
@@ -185,12 +190,12 @@
 
         def spread(w2, q2):
             push(
-                se3.at[two, pl.ds((w2 * 4 + q2) * 16, 16)], r3.at[w, 0, q, two],
-                4, in_mid.at[0], (w2, x, q2),
+                se3.at[two, pl.ds((w2 * 4 + q2) * 16, 16)], r3.at[s, w, 0, q],
+                4, in_me.at[s], (w2, x, q2),
             )
 
         each_far(spread)
-        r3[w, 0, q, two] = se3[two, pl.ds(pl.multiple_of(beta * 16, 16), 16)]
+        r3[s, w, 0, q] = se3[two, pl.ds(pl.multiple_of(beta * 16, 16), 16)]
 
     def stage_two_q(s):
         two = pl.ds(s * 2, 2)
@@ -200,31 +205,58 @@
             sq3[n, :, two] = out[:, n * 128 : n * 128 + 128].reshape(8, 2, 16, 128)
         for d in (2, 1, 3):
             x2 = (x + d) % 4
-            push(sq3.at[x2, :, two], r3.at[:, 1, x, two], 5, in_mid.at[1], (w, x2, q))
-        r3[:, 1, x, two] = sq3[x, :, two]
+            push(sq3.at[x2, :, two], r3.at[s, :, 1, x], 5, in_mq.at[s], (w, x2, q))
+        r3[s, :, 1, x] = sq3[x, :, two]
 
     staged(stage_two_e, stage_two_q, ORDER[1])
 
     rows(b2l, b2f[...])
     columns(b3tc, b3f[...].T)
-
-    await_bytes(se3.at[:, pl.ds(0, 496)], in_mid.at[0])
-    await_bytes(sq3.at[pl.ds(0, 3)], in_mid.at[1])
 
     flat = r3.reshape(8192, 128)
     flat_s = s3.reshape(8192, 128)
     along = e3_ref[pl.ds(x, 1), :]
 
+    def arrived(s):
+        await_bytes(se3.at[pl.ds(0, 2), pl.ds(0, 496)], in_me.at[s])
+        await_bytes(sq3.at[pl.ds(0, 3), :, pl.ds(0, 2)], in_mq.at[s])
+
+    def term(s, pair):
+        for k in range(2):
+            high, low = halves(flat[pl.ds(s * 2048 + pair * 2 + k, 128, stride=16), :])
+            lanes = slice(k * 128, k * 128 + 128)
+            rhs[0:128, lanes] = high
+            rhs[128:256, lanes] = low
+            rhs[256:384, lanes] = high
+        return jnp.dot(b1tm[s], rhs[0:384, :], preferred_element_type=F32)
+
+    def total(at):
+        return flat_s.at[pl.ds(pl.multiple_of(at * DEPTH, DEPTH), DEPTH), :]
+
+    def gather_sum(s, _):
+        arrived(s)
+
+        def one_pair(pair, _):
+            part = term(s, pair)
+            for k in range(2):
+                total(pair * 2 + k)[...] += part[:, k * 128 : k * 128 + 128]
+            return _
+
+        lax.fori_loop(0, 8, one_pair, 0)
+        return _
+
+    lax.fori_loop(0, STEPS - 1, gather_sum, 0)
+    arrived(STEPS - 1)
+
     def middle(pair, _):
-        at = pair * 2
-        rotated = data_right(b1tl, lambda k: flat[pl.ds(at + k, DEPTH, stride=16), :])
-        for k in range(2):
+        part = term(STEPS - 1, pair)
+        for k in range(2):
+            at = pair * 2 + k
             lanes = slice(k * 128, k * 128 + 128)
-            spectrum = e1b[...] * e2_ref[beta * 16 + at + k] * along + noise_ref[0]
-            high, low = halves(rotated[:, lanes] / spectrum)
+            spectrum = e1b[...] * e2_ref[beta * 16 + at] * along + noise_ref[0]
+            high, low = halves((total(at)[...] + part[:, lanes]) / spectrum)
             mid[pair, 0:512, lanes] = high
             mid[pair, 512:1024, lanes] = low
-            mid[pair, 1024:1536, lanes] = high
         return _
 
     lax.fori_loop(0, 8, middle, 0)
@@ -232,7 +264,8 @@
     def back_mid(s, _):
         factor = b1l[pl.ds(pl.multiple_of(s * 128, 128), 128), :]
         for pair in range(8):
-            out = jnp.dot(factor, mid[pair], preferred_element_type=F32)
+            out = jnp.dot(factor[:, 0:1024], mid[pair], preferred_element_type=F32)
+            out += jnp.dot(factor[:, 1024:1536], mid[pair, 0:512], preferred_element_type=F32)
             for k in range(2):
                 flat_s[pl.ds(s * 2048 + pair * 2 + k, 128, stride=16), :] = out[:, k * 128 : k * 128 + 128]
         for d in (2, 1, 3):
@@ -321,29 +354,29 @@
     half = [
         (4, 8, 128, 128), (4, 8, 128, 128), (8, 4, 128, 128), (8, 512, 128),
         (8, 4, 128, 128), (8, 512, 128), (4, 8, 8, 16, 128), (4, 8, 8, 16, 128),
-        (8, 2, 4, 8, 16, 128), (4, 8, 2, 4, 2, 16, 128),
+        (4, 8, 2, 4, 2, 16, 128), (4, 8, 2, 4, 2, 16, 128),
         (8, 512, 128), (8, 4, 128, 128), (4, 8, 128, 128), (4, 8, 128, 128),
         (4, 4, 8, 2, 16, 128), (4, 4, 8, 2, 16, 128), (8, 512, 128), (8, 4, 128, 128),
     ]
     scratch = [pltpu.VMEM(shape, F32) for shape in half]
     scratch += [pltpu.VMEM((512, 512), F32)] * 3
-    scratch += [pltpu.VMEM((1536, 512), BF)] * 2 + [pltpu.VMEM((512, 1536), BF)] * 4
+    scratch += [pltpu.VMEM((1536, 512), BF)] * 2 + [pltpu.VMEM((512, 1536), BF)] * 3 + [pltpu.VMEM((4, 512, 384), BF)]
     scratch += [pltpu.VMEM((256, 1536), BF), pltpu.VMEM((1536, 256), BF)]
-    scratch += [pltpu.VMEM((8, 1536, 256), BF), pltpu.VMEM((512, 128), F32)]
+    scratch += [pltpu.VMEM((8, 1024, 256), BF), pltpu.VMEM((512, 128), F32)]
     dma = pltpu.SemaphoreType.DMA
     scratch += [dma((3,)), dma((12,))] + [dma((STEPS,))] * 4
-    scratch += [dma((2,))] + [dma((STEPS,))] * 4 + [dma((2,))]
+    scratch += [dma((STEPS,))] * 6 + [dma((2,))]
     whole = pl.BlockSpec(memory_space=pl.ANY)
     vmem = pl.BlockSpec(memory_space=pltpu.VMEM)
     smem = pl.BlockSpec(memory_space=pltpu.SMEM)
     return pl.pallas_call(
         kernel,
-        out_shape=jax.ShapeDtypeStruct((64, 128, 128), F32),
+        out_shape=pltpu.VMEM((64, 128, 128), F32),
         in_specs=[whole, whole, whole, whole, vmem, smem, vmem, smem],
-        out_specs=whole,
+        out_specs=vmem,
         scratch_shapes=scratch,
         compiler_params=pltpu.CompilerParams(
-            collective_id=0, has_side_effects=True, vmem_limit_bytes=67043328
+            collective_id=0, has_side_effects=True, vmem_limit_bytes=62500000
         ),
         name="kron_solve",
     )(

time: 174 us -> 172 us (0.989)
  the two profiles are of different devices: /device:TPU:22 before, /device:TPU:100 now
where the time goes in v4:
time: 172 us
  Pallas kernels  169 us (98%)
  local copies, waits for them, and re-layouts  2.02 us (1%)
    pallas_call x1, Pallas kernels, per_device(): pl.pallas_call(kernel, out_shape=pltpu.VMEM((64, 128, 128), F32), in_spec...  169 us

profile of v4, /device:TPU:100, one launch (start us, length us, event | category | flops | bytes accessed | tf_op | source)
XLA Modules:
  0.0 171.5 jit_solution(1490413320889695434)
XLA Ops:
  0.7 168.9 %kron_solve.1 = f32[64,128,128]{2,1,0:T(8,128)S(1)} custom-call(f32[64,128,128]{2,1,0:T(8,128)} %t_ref.1, f32[512,512]{1,0:T(8,128)} %b1_ref.1, f32[512,512]{1,0:T(8,128)} %b2_ref.1, f32[512,512]{1,0:T(8,128)} %b3_ref.1, f32[1,512]{1,0:T(1,128)} %bitcast.2, f32[512]{0:T(512)} %e2_ref.1, f32[4,128]{1,0:T(4,128)} %bitcast.3, f32[1]{0:T(128)S(6)} %copy.11.noise_ref), custom_call_target="tpu_custom_call" | custom-call | tf_op jit(solution)/shard_map/kron_solve/pallas_call | solution.py:372
  169.5 2.0 %copy.10 = f32[64,128,128]{2,1,0:T(8,128)} copy(f32[64,128,128]{2,1,0:T(8,128)S(1)} %kron_solve.1) | data formatting | bytes 8388608

commit v5 on v4

--- a/solution.py
+++ b/solution.py
@@ -12,7 +12,7 @@
 F32 = jnp.float32
 STEPS = 4
 DEPTH = 512
-ORDER = ("qe", "eq", "eq", "eq")
+ORDER = ("q|e", "eq", "eq", "eq")
 
 
 def halves(value):
@@ -63,13 +63,14 @@
     def await_bytes(ref, sem):
         pltpu.make_async_copy(ref, ref, sem).wait()
 
-    def staged(part_e, part_q, order):
-        def body(s, _):
-            for part in order:
-                (part_e if part == "e" else part_q)(s)
-            return _
-
-        lax.fori_loop(0, STEPS, body, 0)
+    def staged(part_e, part_q, orders):
+        for order in orders.split("|"):
+            def body(s, _):
+                for part in order:
+                    (part_e if part == "e" else part_q)(s)
+                return _
+
+            lax.fori_loop(0, STEPS, body, 0)
 
     loads = [
         pltpu.make_async_copy(ref, buf, base_sem.at[n])
@@ -180,6 +181,19 @@
         b1tm[n, :, 256:384] = low[:, n * 128 : n * 128 + 128]
     s3[...] = jnp.zeros_like(s3)
     e1b[...] = jnp.broadcast_to(e1_ref[...], (128, DEPTH)).T
+    along = e3_ref[pl.ds(x, 1), :]
+    inverse = (se1p.reshape(4096, 128), sq1p.reshape(4096, 128))
+
+    def column(at):
+        return pl.ds(pl.multiple_of(at * DEPTH, DEPTH), DEPTH)
+
+    def invert(pair, _):
+        for k in range(2):
+            spectrum = e1b[...] * e2_ref[beta * 16 + pair * 2 + k] * along + noise_ref[0]
+            inverse[k][column(pair), :] = 1.0 / spectrum
+        return _
+
+    lax.fori_loop(0, 8, invert, 0)
 
     def stage_two_e(s):
         two = pl.ds(s * 2, 2)
@@ -215,8 +229,6 @@
 
     flat = r3.reshape(8192, 128)
     flat_s = s3.reshape(8192, 128)
-    along = e3_ref[pl.ds(x, 1), :]
-
     def arrived(s):
         await_bytes(se3.at[pl.ds(0, 2), pl.ds(0, 496)], in_me.at[s])
         await_bytes(sq3.at[pl.ds(0, 3), :, pl.ds(0, 2)], in_mq.at[s])
@@ -231,7 +243,7 @@
         return jnp.dot(b1tm[s], rhs[0:384, :], preferred_element_type=F32)
 
     def total(at):
-        return flat_s.at[pl.ds(pl.multiple_of(at * DEPTH, DEPTH), DEPTH), :]
+        return flat_s.at[column(at), :]
 
     def gather_sum(s, _):
         arrived(s)
@@ -253,8 +265,7 @@
         for k in range(2):
             at = pair * 2 + k
             lanes = slice(k * 128, k * 128 + 128)
-            spectrum = e1b[...] * e2_ref[beta * 16 + at] * along + noise_ref[0]
-            high, low = halves((total(at)[...] + part[:, lanes]) / spectrum)
+            high, low = halves((total(at)[...] + part[:, lanes]) * inverse[k][column(pair), :])
             mid[pair, 0:512, lanes] = high
             mid[pair, 512:1024, lanes] = low
         return _

time: 172 us -> 167 us (0.971)
  the two profiles are of different devices: /device:TPU:100 before, /device:TPU:26 now
where the time goes in v5:
time: 167 us
  Pallas kernels  164 us (98%)
  local copies, waits for them, and re-layouts  2.02 us (1%)
    pallas_call x1, Pallas kernels, per_device(): pl.pallas_call(kernel, out_shape=pltpu.VMEM((64, 128, 128), F32), in_spec...  164 us

profile of v5, /device:TPU:26, one launch (start us, length us, event | category | flops | bytes accessed | tf_op | source)
XLA Modules:
  0.0 167.0 jit_solution(17689227634538389527)
XLA Ops:
  0.7 164.3 %kron_solve.1 = f32[64,128,128]{2,1,0:T(8,128)S(1)} custom-call(f32[64,128,128]{2,1,0:T(8,128)} %t_ref.1, f32[512,512]{1,0:T(8,128)} %b1_ref.1, f32[512,512]{1,0:T(8,128)} %b2_ref.1, f32[512,512]{1,0:T(8,128)} %b3_ref.1, f32[1,512]{1,0:T(1,128)} %bitcast.2, f32[512]{0:T(512)} %e2_ref.1, f32[4,128]{1,0:T(4,128)} %bitcast.3, f32[1]{0:T(128)S(6)} %copy.11.noise_ref), custom_call_target="tpu_custom_call" | custom-call | tf_op jit(solution)/shard_map/kron_solve/pallas_call | solution.py:383
  164.9 2.0 %copy.10 = f32[64,128,128]{2,1,0:T(8,128)} copy(f32[64,128,128]{2,1,0:T(8,128)S(1)} %kron_solve.1) | data formatting | bytes 8388608

commit v6 on v5

--- a/solution.py
+++ b/solution.py
@@ -270,32 +270,41 @@
             mid[pair, 512:1024, lanes] = low
         return _
 
-    lax.fori_loop(0, 8, middle, 0)
+    def turn(s, pair):
+        factor = b1l[pl.ds(pl.multiple_of(s * 128, 128), 128), :]
+        out = jnp.dot(factor[:, 0:1024], mid[pair], preferred_element_type=F32)
+        out += jnp.dot(factor[:, 1024:1536], mid[pair, 0:512], preferred_element_type=F32)
+        for k in range(2):
+            flat_s[pl.ds(s * 2048 + pair * 2 + k, 128, stride=16), :] = out[:, k * 128 : k * 128 + 128]
+
+    def send_back(s, low, count):
+        some = pl.ds(low, count)
+        mine = pl.ds(pl.multiple_of(beta * 16 + low, 8), count)
+        two = pl.ds(s * 2, 2)
+        for d in (2, 1, 3):
+            x2 = (x + d) % 4
+            push(s3.at[s, :, 1, x2, :, some], rq3p.at[x, s, :, :, some], 6, in_q3p.at[s], (w, x2, q))
+
+        def spread(w2, q2):
+            push(s3.at[s, w2, 0, q2, :, some], re3p.at[two, mine], 7, in_e3p.at[s], (w2, x, q2))
+
+        each_far(spread)
+        rq3p[x, s, :, :, some] = s3[s, :, 1, x, :, some]
+        re3p[two, mine] = s3[s, w, 0, q, :, some]
+
+    for part in range(2):
+        lax.fori_loop(part * 4, part * 4 + 4, middle, 0)
+        for pair in range(part * 4, part * 4 + 4):
+            turn(0, pair)
+        send_back(0, part * 8, 8)
 
     def back_mid(s, _):
-        factor = b1l[pl.ds(pl.multiple_of(s * 128, 128), 128), :]
         for pair in range(8):
-            out = jnp.dot(factor[:, 0:1024], mid[pair], preferred_element_type=F32)
-            out += jnp.dot(factor[:, 1024:1536], mid[pair, 0:512], preferred_element_type=F32)
-            for k in range(2):
-                flat_s[pl.ds(s * 2048 + pair * 2 + k, 128, stride=16), :] = out[:, k * 128 : k * 128 + 128]
-        for d in (2, 1, 3):
-            x2 = (x + d) % 4
-            push(s3.at[s, :, 1, x2], rq3p.at[x, s], 6, in_q3p.at[s], (w, x2, q))
-
-        def spread(w2, q2):
-            push(
-                s3.at[s, w2, 0, q2],
-                re3p.at[pl.ds(s * 2, 2), pl.ds(pl.multiple_of(beta * 16, 16), 16)],
-                7, in_e3p.at[s], (w2, x, q2),
-            )
-
-        each_far(spread)
-        rq3p[x, s] = s3[s, :, 1, x]
-        re3p[pl.ds(s * 2, 2), pl.ds(pl.multiple_of(beta * 16, 16), 16)] = s3[s, w, 0, q]
+            turn(s, pair)
+        send_back(s, 0, 16)
         return _
 
-    lax.fori_loop(0, STEPS, back_mid, 0)
+    lax.fori_loop(1, STEPS, back_mid, 0)
 
     def back_one_e(s):
         two = pl.ds(s * 2, 2)

time: 167 us -> 164 us (0.982)
  the two profiles are of different devices: /device:TPU:26 before, /device:TPU:120 now
where the time goes in v6:
time: 164 us
  Pallas kernels  161 us (98%)
  local copies, waits for them, and re-layouts  2.02 us (1%)
    pallas_call x1, Pallas kernels, per_device(): pl.pallas_call(kernel, out_shape=pltpu.VMEM((64, 128, 128), F32), in_spec...  161 us

profile of v6, /device:TPU:120, one launch (start us, length us, event | category | flops | bytes accessed | tf_op | source)
XLA Modules:
  0.0 164.0 jit_solution(2490550567670440978)
XLA Ops:
  0.7 161.4 %kron_solve.1 = f32[64,128,128]{2,1,0:T(8,128)S(1)} custom-call(f32[64,128,128]{2,1,0:T(8,128)} %t_ref.1, f32[512,512]{1,0:T(8,128)} %b1_ref.1, f32[512,512]{1,0:T(8,128)} %b2_ref.1, f32[512,512]{1,0:T(8,128)} %b3_ref.1, f32[1,512]{1,0:T(1,128)} %bitcast.2, f32[512]{0:T(512)} %e2_ref.1, f32[4,128]{1,0:T(4,128)} %bitcast.3, f32[1]{0:T(128)S(6)} %copy.11.noise_ref), custom_call_target="tpu_custom_call" | custom-call | tf_op jit(solution)/shard_map/kron_solve/pallas_call | solution.py:392
  162.0 2.0 %copy.10 = f32[64,128,128]{2,1,0:T(8,128)} copy(f32[64,128,128]{2,1,0:T(8,128)S(1)} %kron_solve.1) | data formatting | bytes 8388608

commit v7 on v6

--- a/solution.py
+++ b/solution.py
@@ -12,7 +12,7 @@
 F32 = jnp.float32
 STEPS = 4
 DEPTH = 512
-ORDER = ("q|e", "eq", "eq", "eq")
+ORDER = ("q|e", "eq", "eq", "q|e")
 
 
 def halves(value):
@@ -113,10 +113,10 @@
         target[:, 512:1024] = high
         target[:, 1024:1536] = low
 
+    loads[1].wait()
+    rows(b2tl, b2f[...].T)
     loads[0].wait()
     columns(b3c, b3f[...])
-    loads[1].wait()
-    rows(b2tl, b2f[...].T)
 
     def data_left(piece, factor):
         for k in range(4):

time: 164 us -> 165 us (level)
  the two profiles are of different devices: /device:TPU:120 before, /device:TPU:33 now
where the time goes in v7:
time: 165 us; the launch traced here: 162 us
  Pallas kernels  160 us (97%)
  local copies, waits for them, and re-layouts  2.02 us (1%)
    pallas_call x1, Pallas kernels, per_device(): pl.pallas_call(kernel, out_shape=pltpu.VMEM((64, 128, 128), F32), in_spec...  160 us

profile of v7, /device:TPU:33, one launch (start us, length us, event | category | flops | bytes accessed | tf_op | source)
XLA Modules:
  0.0 162.5 jit_solution(17562419464406599508)
XLA Ops:
  0.7 159.8 %kron_solve.1 = f32[64,128,128]{2,1,0:T(8,128)S(1)} custom-call(f32[64,128,128]{2,1,0:T(8,128)} %t_ref.1, f32[512,512]{1,0:T(8,128)} %b1_ref.1, f32[512,512]{1,0:T(8,128)} %b2_ref.1, f32[512,512]{1,0:T(8,128)} %b3_ref.1, f32[1,512]{1,0:T(1,128)} %bitcast.2, f32[512]{0:T(512)} %e2_ref.1, f32[4,128]{1,0:T(4,128)} %bitcast.3, f32[1]{0:T(128)S(6)} %copy.11.noise_ref), custom_call_target="tpu_custom_call" | custom-call | tf_op jit(solution)/shard_map/kron_solve/pallas_call | solution.py:392
  160.5 2.0 %copy.10 = f32[64,128,128]{2,1,0:T(8,128)} copy(f32[64,128,128]{2,1,0:T(8,128)S(1)} %kron_solve.1) | data formatting | bytes 8388608
